TPU v7x, 8 devices: a whole 2x2x1 slice. The times are simulated.
8 devices in a mesh: dz: 2 (over z, y), dy: 2 (over x), dx: 2 (over core).
Axes of the slice: x: 2, y: 2, z: 1, core: 2. Of those that a mesh axis runs over, the one named last changes fastest.
Arguments:
- g_emb: float32 [8, 2048, 768], P(('dz', 'dy', 'dx'))
- g_attn: float32 [8, 1, 4, 768, 768], P(('dz', 'dy', 'dx'))
- g_in: float32 [8, 1, 768, 3072], P(('dz', 'dy', 'dx'))
- g_out: float32 [8, 1, 3072, 768], P(('dz', 'dy', 'dx'))
- g_vecd: float32 [8, 1, 9, 768], P(('dz', 'dy', 'dx'))
- g_vecf: float32 [8, 1, 3072], P(('dz', 'dy', 'dx'))
- opt_m: float32 [8660992], P(('dz', 'dy', 'dx'))
- opt_v: float32 [8660992], P(('dz', 'dy', 'dx'))
- master: float32 [8660992], P(('dz', 'dy', 'dx'))
- tok_ids: int32 [131072], P(('dz', 'dy', 'dx'))
- act_in: bfloat16 [131072, 768], P(('dz', 'dy', 'dx'))
Outputs:
- output 1: float32 [8660992], P(('dz', 'dy', 'dx'))
- output 2: float32 [8660992], P(('dz', 'dy', 'dx'))
- output 3: float32 [8660992], P(('dz', 'dy', 'dx'))
- output 4: bfloat16 [2048, 768], replicated
- output 5: bfloat16 [1, 4, 768, 768], replicated
- output 6: bfloat16 [1, 768, 3072], replicated
- output 7: bfloat16 [1, 3072, 768], replicated
- output 8: bfloat16 [1, 9, 768], replicated
- output 9: bfloat16 [1, 3072], replicated
- output 10: bfloat16 [131072, 768], P(('dz', 'dy', 'dx'))
All inputs are finite; a program needn't handle non-finite values.
Results may differ from a plain program's by a relative error of at most 0.001.
Values are sent between devices in bfloat16 or wider.
A program may use at most 1 GiB of HBM per device.

v0:
```python
import math
import jax
import jax.numpy as jnp
from jax import lax
from jax.sharding import PartitionSpec as P

LEARN_RATE = 0.002
BETA_ONE = 0.9
BETA_TWO = 0.95
ADAM_EPS = 1e-8
ADAM_STEP = 2
AXES = ("dz", "dy", "dx")
GRAD_RANKS = (3, 5, 4, 4, 4, 3)


def adam_update(grad_vals, opt_m, opt_v, master):
    m_new = BETA_ONE * opt_m + (1.0 - BETA_ONE) * grad_vals
    v_new = BETA_TWO * opt_v + (1.0 - BETA_TWO) * grad_vals * grad_vals
    m_hat = m_new / (1.0 - BETA_ONE ** ADAM_STEP)
    v_hat = v_new / (1.0 - BETA_TWO ** ADAM_STEP)
    w_new = master - LEARN_RATE * m_hat / (jnp.sqrt(v_hat) + ADAM_EPS)
    return m_new, v_new, w_new


def split_flat(flat_vals, shapes):
    pieces = []
    offset = 0
    for tensor_shape in shapes:
        elem_count = math.prod(tensor_shape)
        pieces.append(flat_vals[offset:offset + elem_count].reshape(tensor_shape))
        offset = offset + elem_count
    return pieces


def ffn_block(wb_emb, w_in, b_in, w_out, b_out, tok_ids, act_in):
    emb_rows = jnp.take(wb_emb, tok_ids, axis=0).astype(jnp.float32)
    hidden = (emb_rows * math.sqrt(wb_emb.shape[1]) + act_in.astype(jnp.float32)).astype(jnp.bfloat16)
    pre_act = jnp.dot(hidden, w_in, preferred_element_type=jnp.float32) + b_in.astype(jnp.float32)
    inner_act = jax.nn.gelu(pre_act, approximate=True).astype(jnp.bfloat16)
    return (jnp.dot(inner_act, w_out, preferred_element_type=jnp.float32) + b_out.astype(jnp.float32)).astype(jnp.bfloat16)


def solution(mesh):
    devices = math.prod([mesh.shape[axis_name] for axis_name in AXES])

    def device_step(g_emb, g_attn, g_in, g_out, g_vecd, g_vecf, opt_m, opt_v, master, tok_ids, act_in):
        grad_list = [g_emb, g_attn, g_in, g_out, g_vecd, g_vecf]
        shapes = [grad_arr.shape[1:] for grad_arr in grad_list]
        param_count = sum(math.prod(tensor_shape) for tensor_shape in shapes)
        shard_len = opt_m.shape[0]
        local_flat = jnp.concatenate([grad_arr.reshape(-1) for grad_arr in grad_list])
        local_flat = jnp.pad(local_flat, (0, shard_len * devices - param_count))
        grad_shard = lax.psum_scatter(local_flat, AXES, scatter_dimension=0, tiled=True) / devices
        m_new, v_new, w_new = adam_update(grad_shard, opt_m, opt_v, master)
        full_half = lax.all_gather(w_new.astype(jnp.bfloat16), AXES, axis=0, tiled=True)
        wb_emb, wb_attn, wb_in, wb_out, wb_vecd, wb_vecf = split_flat(full_half, shapes)
        y_out = ffn_block(wb_emb, wb_in[0], wb_vecf[0], wb_out[0], wb_vecd[0, 8], tok_ids, act_in)
        return (m_new, v_new, w_new, wb_emb, wb_attn, wb_in, wb_out, wb_vecd, wb_vecf, y_out)

    grad_specs = tuple(P(AXES, *([None] * (grad_rank - 1))) for grad_rank in GRAD_RANKS)
    in_specs = grad_specs + (P(AXES), P(AXES), P(AXES), P(AXES), P(AXES, None))
    out_specs = (P(AXES), P(AXES), P(AXES), P(), P(), P(), P(), P(), P(), P(AXES, None))
    return jax.shard_map(device_step, mesh=mesh, in_specs=in_specs, out_specs=out_specs, check_vma=False)
```

profile of v0, /device:TPU:0, one launch (start us, length us, event | category | flops | bytes accessed | tf_op | source)
XLA Modules:
  0.0 1410.3 jit_solution(6013701191268099110)
XLA Ops:
  7.2 0.0 all-reduce.4.cloned.1.call-start
  7.2 0.8 reduce
  8.1 6.9 reshape.69
  15.0 10.7 reshape.70
  25.7 9.5 copy.21
  35.2 10.8 reshape.72
  45.9 3.1 constant_dynamic-update-slice_fusion.5
  49.0 4.7 constant_dynamic-update-slice_fusion.4
  53.7 0.0 copy-start.3
  53.8 4.7 constant_dynamic-update-slice_fusion.3
  58.5 4.7 constant_dynamic-update-slice_fusion.2
  63.3 0.0 copy-done.3
  63.3 12.0 pad.4
  75.3 0.0 all-reduce.4.cloned.1.call-update
  75.3 0.2 all-gather.3.cloned.1.call-start
  75.6 0.0 copy-start.1
  75.6 401.0 %all-reduce.4.cloned.1.call-done = f32[8660992]{0:T(1024)} async-done(((f32[8660992]{0:T(1024)}), f32[8660992]{0:T(1024)}) %all-reduce.4.cloned.1.call-update) | async-done | bytes 34643984
  476.6 10.5 fusion.22
  487.1 25.4 %reshape.91 = bf16[1,1,1082624]{2,1,0:T(2,128)(2,1)} reshape(bf16[1082624]{0:T(1024)(128)(2,1)S(1)} %get-tuple-element.10) | data formatting | bytes 4330496
  512.5 0.0 all-gather.3.cloned.1.call-update
  512.5 0.0 copy-done.1
  512.6 161.1 %all-gather.3.cloned.1.call-done = bf16[8,1,1082624]{2,1,0:T(2,128)(2,1)} async-done(((bf16[1,1,1082624]{2,1,0:T(2,128)(2,1)}), bf16[8,1,1082624]{2,1,0:T(2,128)(2,1)}) %all-gather.3.cloned.1.call-update) | async-done | bytes 17322000 | tf_op jit(solution)/shard_map/all_gather | solution.py:55
  673.7 333.6 %reduce.1 = bf16[8,1082624]{1,0:T(8,128)(2,1)} reduce(bf16[8,1,1082624]{2,1,0:T(2,128)(2,1)} %all-gather.3.cloned.1.call-done, bf16[]{:T(256)} %constant.64), dimensions={1}, to_apply=%all-gather.reduce_sub_computation | reduce | bytes 34643968 | tf_op jit(solution)/shard_map/all_gather | solution.py:55
  1007.4 38.0 %reshape.92 = bf16[8660992]{0:T(1024)(128)(2,1)} reshape(bf16[8,1082624]{1,0:T(8,128)(2,1)} %reduce.1) | data formatting | bytes 34643968
  1045.4 0.7 slice_convert_fusion.1
  1046.1 3.2 slice.30
  1049.3 10.8 fusion.23
  1060.1 0.0 slice-start
  1060.1 9.3 squeeze_reshape.7
  1069.3 9.2 reshape.78
  1078.6 8.2 squeeze_reshape.6
  1086.8 8.2 reshape.77
  1095.0 0.0 slice-done
  1095.0 0.0 copy-start.2
  1095.0 0.6 fusion.13
  1095.6 0.0 copy-done.2
  1095.6 0.6 reshape.80
  1096.2 5.1 reshape.75
  1101.4 0.0 copy-start
  1101.4 9.6 reshape.76
  1111.0 67.8 %gather_fusion = bf16[16384,768]{1,0:T(8,128)(2,1)} fusion(bf16[2048,768]{1,0:T(8,128)(2,1)S(1)} %reshape.75, s32[16384]{0:T(1024)S(1)} %fusion.12), kind=kCustom, calls=%fused_computation | custom fusion | bytes 50397184 | tf_op jit(solution)/shard_map/jit(_take)/gather | solution.py:36
  1178.8 0.0 copy-done
  1178.8 0.0 copy-start.4
  1178.8 136.4 %fusion.7.clone.4 = bf16[16384,3072]{1,0:T(8,128)(2,1)} fusion(bf16[768,3072]{1,0:T(8,128)(2,1)} %squeeze_reshape.6, f32[3072]{0:T(1024)S(1)} %get-tuple-element.14, bf16[16384,768]{1,0:T(8,128)(2,1)} %param.21, bf16[16384,768]{1,0:T(8,128)(2,1)} %gather_fusion, pred[16384]{0:T(1024)(128)(4,1)S(1)} %compare_and_fusion), kind=kOutput, calls=%fused_computation.9.clone.clone.clone.1 | convolution fusion | flops 77888225280 | bytes 155742208 | tf_op jit(solution)/shard_map/dot_general | solution.py:38
  1315.2 0.0 copy-done.4
  1315.2 88.0 %add_convert_fusion = bf16[16384,768]{1,0:T(8,128)(2,1)} fusion(bf16[3072,768]{1,0:T(8,128)(2,1)} %squeeze_reshape.7, f32[768]{0:T(1024)S(1)} %copy-done.4, bf16[16384,3072]{1,0:T(8,128)(2,1)} %fusion.7.clone.4), kind=kOutput, calls=%fused_computation.10 | convolution fusion | flops 77334577152 | bytes 130550784 | tf_op jit(solution)/shard_map/dot_general | solution.py:40
  (6 shorter events, 0.1 us)
Async XLA Ops:
  7.2 469.4 %all-reduce.4.cloned.1.call-start = ((), (), s32[]{:S(2)}) async-start(), calls=%async_computation.1 | async-start | bytes 69287936
  53.7 9.5 copy-start.3
  75.3 598.4 %all-gather.3.cloned.1.call-start = ((), (), s32[]{:S(2)}) async-start(), calls=%async_computation | async-start | bytes 38974464 | tf_op jit(solution)/shard_map/all_gather | solution.py:55
  75.6 437.0 %copy-start.1 = (s32[16384]{0:T(1024)S(1)}, s32[16384]{0:T(1024)}, u32[]{:S(2)}) copy-start(s32[16384]{0:T(1024)} %param.20) | copy-start | bytes 196612
  1060.1 34.9 %slice-start = ((bf16[8660992]{0:T(1024)(128)(2,1)}), bf16[6912]{0:T(1024)(128)(2,1)S(1)}, s32[]{:S(2)}) async-start(bf16[8660992]{0:T(1024)(128)(2,1)} %reshape.92), calls=%async_computation.2 | async-start | bytes 28672 | tf_op jit(solution)/shard_map/slice | solution.py:30
  1095.0 0.6 copy-start.2
  1101.4 77.5 %copy-start = (bf16[2048,768]{1,0:T(8,128)(2,1)}, bf16[2048,768]{1,0:T(8,128)(2,1)S(1)}, u32[]{:S(2)}) copy-start(bf16[2048,768]{1,0:T(8,128)(2,1)S(1)} %reshape.75) | copy-start | bytes 9437188
  1178.8 136.4 %copy-start.4 = (f32[768]{0:T(1024)S(1)}, f32[768]{0:T(1024)}, u32[]{:S(2)}) copy-start(f32[768]{0:T(1024)} %fusion.13) | copy-start | bytes 9220
Sparse Core Ops, SparseCore 0:
  75.5 401.0 all-reduce.3
  512.7 161.0 all-gather.2
where the time goes:
time: 1420 us; the launch traced here: 1410 us
  waiting for transfers between devices  562 us (40%)
  other arithmetic  346 us (24%)
  local copies, waits for them, and re-layouts  263 us (19%)
  matrix products  224 us (16%)
  between operations  14.5 us (1%)
    unnamed x3, waiting for transfers between devices  401 us
    all_gather x1, other arithmetic, device_step(): lax.all_gather(w_new.astype(jnp.bfloat16), AXES, axis=0, tiled=True)  334 us
    all_gather x1, waiting for transfers between devices, device_step(): lax.all_gather(w_new.astype(jnp.bfloat16), AXES, axis=0, tiled=True)  161 us
    dot_general x1, matrix products, ffn_block(): jnp.dot(hidden, w_in, preferred_element_type=jnp.float32)  136 us
    unnamed x18, local copies, waits for them, and re-layouts  90.3 us
    dot_general x1, matrix products, ffn_block(): jnp.dot(inner_act, w_out, preferred_element_type=jnp.float32)  88 us
    gather x1, local copies, waits for them, and re-layouts, ffn_block(): emb_rows = jnp.take(wb_emb, tok_ids, axis=0).astype(jnp.float32)  67.8 us
    reshape x6, local copies, waits for them, and re-layouts, split_flat(): pieces.append(flat_vals[offset:offset + elem_count].reshape(tensor_shape))  32.8 us
  transfers between devices with their start and end apart: 2, of which 2 were waited for; matrix products, arithmetic and copies ran while one was open for 0% of the time, Pallas kernels for 0%

commit v1 on v0

v1 whole, which is shorter than its diff:
```python
import functools
import math
import jax
import jax.numpy as jnp
from jax import lax
from jax.experimental import pallas as pl
from jax.experimental.pallas import tpu as pltpu
from jax.sharding import PartitionSpec as P

LEARN_RATE = 0.002
BETA_ONE = 0.9
BETA_TWO = 0.95
ADAM_EPS = 1e-8
ADAM_STEP = 2
AXES = ("dz", "dy", "dx")
GRAD_RANKS = (3, 5, 4, 4, 4, 3)
MESH = pl.DeviceIdType.MESH

D = 768
FF = 3072
VOCAB = 2048
NCH = 11
TPC = 96
CROWS = 768
PART = NCH * CROWS
OWN = 8458
HEAD = 80
BOUNDS = (0, 16, 40, 64, 88)


def adam_math(grad, m_old, v_old, w_old):
    m_new = BETA_ONE * m_old + (1.0 - BETA_ONE) * grad
    v_new = BETA_TWO * v_old + (1.0 - BETA_TWO) * grad * grad
    m_hat = m_new / (1.0 - BETA_ONE ** ADAM_STEP)
    v_hat = v_new / (1.0 - BETA_TWO ** ADAM_STEP)
    w_new = w_old - LEARN_RATE * m_hat / (jnp.sqrt(v_hat) + ADAM_EPS)
    return m_new, v_new, w_new


def comm_kernel(g_emb, g_attn, g_in, g_out, m_in, v_in, w_in, frag, vec,
                m_out, v_out, w_out, wb_all, wvec_out,
                rc, own, r1, r2, g_flat, w_flat, m_vm, v_vm, w_vm, wbuf, vecs, wvec,
                d2d_s, d2d_r, own_sem, s1_s, s1_r, s2_s, s2_r,
                as_s, as_r, af_s, af_r, ac_s, ac_r, wloc, ld_sem, st_sem,
                fr_s, fr_r, gt_s, gt_r, vc_s, vc_r, wv_s, wv_r, wv_loc):
    dz, dy, dx = lax.axis_index("dz"), lax.axis_index("dy"), lax.axis_index("dx")
    me = dz * 4 + dy * 2 + dx
    first = jnp.where(dx == 0, dz, dy)
    second = jnp.where(dx == 0, dy, dz)
    p_first = (jnp.where(dx == 0, 1 - dz, dz), jnp.where(dx == 0, dy, 1 - dy), dx)
    p_second = (jnp.where(dx == 0, dz, 1 - dz), jnp.where(dx == 0, 1 - dy, dy), dx)
    p_core = (dz, dy, 1 - dx)

    def coords(index):
        return (index // 4, lax.rem(index // 2, 2), lax.rem(index, 2))

    def part_of(core, a, b):
        f = jnp.where(core == 0, dz, dy)
        s = jnp.where(core == 0, dy, dz)
        f = f if a == 0 else 1 - f
        s = s if b == 0 else 1 - s
        return jnp.where(core == 0, f * 4 + s * 2, s * 4 + f * 2 + 1)

    mine = [part_of(dx, a, b) for a in (0, 1) for b in (0, 1)]
    theirs = [part_of(1 - dx, a, b) for a in (0, 1) for b in (0, 1)]
    shift = me * 10

    barrier = pltpu.get_barrier_semaphore()
    for other in range(1, 8):
        pl.semaphore_signal(barrier, inc=1, device_id=coords(lax.rem(me + other, 8)), device_id_type=MESH)

    loads = []
    for n, (src, dst) in enumerate(((m_in, m_vm), (v_in, v_vm), (w_in, w_vm))):
        loads.append(pltpu.make_async_copy(src, dst.at[pl.ds(HEAD, OWN)], ld_sem.at[n]))
        loads[-1].start()

    def from_grad(part, j, go):
        gchunk = part * NCH + j
        for n, ref in enumerate((g_emb, g_attn, g_in, g_out)):
            @pl.when((gchunk >= BOUNDS[n]) & (gchunk < BOUNDS[n + 1]))
            def _():
                go(ref.at[pl.ds((gchunk - BOUNDS[n]) * TPC, TPC)])

    def own_load(j):
        slot = lax.rem(j, 2)
        for q in range(4):
            from_grad(mine[q], j, lambda src: pltpu.make_async_copy(src, own.at[slot, q], own_sem.at[slot, q]).start())

    def d2d(j, q, src):
        return pltpu.make_async_remote_copy(
            src_ref=src, dst_ref=rc.at[j, q], send_sem=d2d_s.at[j, q], recv_sem=d2d_r.at[j, q],
            device_id=p_core, device_id_type=MESH)

    def d2d_send(j):
        for q in range(4):
            from_grad(theirs[q], j, lambda src: d2d(j, q, src).start())

    def step_one(j):
        return pltpu.make_async_remote_copy(
            src_ref=rc.at[j, pl.ds(2, 2)], dst_ref=r1.at[j], send_sem=s1_s.at[j], recv_sem=s1_r.at[j],
            device_id=p_first, device_id_type=MESH)

    def step_two(j):
        return pltpu.make_async_remote_copy(
            src_ref=r1.at[j, 1], dst_ref=r2.at[j], send_sem=s2_s.at[j], recv_sem=s2_r.at[j],
            device_id=p_second, device_id_type=MESH)

    def gather(j, part, src, target, sends, recvs):
        return pltpu.make_async_remote_copy(
            src_ref=src, dst_ref=wb_all.at[part * NCH + j], send_sem=sends, recv_sem=recvs,
            device_id=target, device_id_type=MESH)

    def frag_copy(n, dst):
        return pltpu.make_async_remote_copy(
            src_ref=frag.at[pl.ds(HEAD * n, HEAD)], dst_ref=dst.at[pl.ds(0, HEAD)],
            send_sem=fr_s.at[n], recv_sem=fr_r.at[n],
            device_id=coords(jnp.minimum(me + 1, 7)), device_id_type=MESH)

    def tail_copy():
        return pltpu.make_async_remote_copy(
            src_ref=g_flat.at[pl.ds(HEAD, 80)], dst_ref=g_flat.at[pl.ds(HEAD + PART, 80)],
            send_sem=gt_s, recv_sem=gt_r,
            device_id=coords(jnp.maximum(me - 1, 0)), device_id_type=MESH)

    def vec_copy(index):
        return pltpu.make_async_remote_copy(
            src_ref=vec, dst_ref=vecs.at[index], send_sem=vc_s, recv_sem=vc_r.at[index],
            device_id=coords(jnp.int32(7)), device_id_type=MESH)

    def wvec_copy(n):
        return pltpu.make_async_remote_copy(
            src_ref=wvec, dst_ref=wvec, send_sem=wv_s.at[n], recv_sem=wv_r,
            device_id=coords(jnp.int32(n)), device_id_type=MESH)

    def out_copies(row, rows, n0):
        return [pltpu.make_async_copy(src.at[pl.ds(HEAD + row, rows)], dst.at[pl.ds(row, rows)], st_sem.at[n0, n])
                for n, (src, dst) in enumerate(((m_vm, m_out), (v_vm, v_out), (w_vm, w_out)))]

    own_load(0)
    own_load(1)
    pl.semaphore_wait(barrier, 7)
    for j in range(3):
        d2d_send(jnp.int32(j))

    @pl.when(me < 7)
    def _():
        for n, dst in enumerate((m_vm, v_vm, w_vm)):
            frag_copy(n, dst).start()
        vec_copy(me).start()

    def add_tiles(dst, src, tiles, per):
        def body(i, _):
            at = pl.ds(i * per, per)
            dst[at] = dst[at] + src[at]
            return 0
        lax.fori_loop(0, tiles // per, body, 0)

    def stage_a(j):
        slot = lax.rem(j, 2)

        @pl.when(j + 3 < NCH)
        def _():
            d2d_send(j + 3)
        for q in (2, 3, 0, 1):
            pltpu.make_async_copy(own.at[slot, q], own.at[slot, q], own_sem.at[slot, q]).wait()
            d2d(j, q, rc.at[j, q]).wait_recv()
            add_tiles(rc.at[j, q], own.at[slot, q], TPC, 8)
            if q == 3:
                step_one(j).start()

        @pl.when(j + 2 < NCH)
        def _():
            own_load(j + 2)

    def stage_b(j):
        step_one(j).wait_recv()
        add_tiles(r1.at[j, 1], rc.at[j, 1], TPC, 8)
        step_two(j).start()
        add_tiles(r1.at[j, 0], rc.at[j, 0], TPC, 8)

    def adam_rows(t, rows, store):
        at = pl.ds(pl.multiple_of(t, 8), rows)
        moved = pl.ds(t + shift, rows)
        m_new, v_new, w_new = adam_math(g_flat[moved, :], m_vm[at, :], v_vm[at, :], w_vm[at, :])
        if store:
            m_vm[at, :] = m_new
            v_vm[at, :] = v_new
            w_vm[at, :] = w_new
        w_flat[moved, :] = w_new

    def tail_sums():
        @pl.when(me < 7)
        def _():
            tail_copy().wait_recv()

        @pl.when(me == 7)
        def _():
            for n in range(7):
                vec_copy(n).wait_recv()
            pltpu.make_async_copy(vec, vecs.at[7], wv_loc).start()
            pltpu.make_async_copy(vec, vecs.at[7], wv_loc).wait()
            total = vecs[0]
            for n in range(1, 8):
                total = total + vecs[n]
            g_flat[pl.ds(HEAD + PART, 80), :] = total * 0.125

    def stage_c(j):
        step_two(j).wait_recv()
        gchunk = me * NCH + j
        is_in = (gchunk >= BOUNDS[2]) & (gchunk < BOUNDS[3])
        base = HEAD + j * CROWS

        def to_flat(width, bands):
            def body(b, _):
                for c in range(width):
                    i = b * width + c
                    g_flat[pl.ds(base + b * (8 * width) + c, 8, stride=width), :] = (r2[j, i] + r1[j, 0, i]) * 0.125
                return 0
            lax.fori_loop(0, bands, body, 0)

        def to_tiles(width, bands):
            def body(b, _):
                for c in range(width):
                    rows = w_flat[pl.ds(base + b * (8 * width) + c, 8, stride=width), :]
                    wbuf[j, b * width + c] = rows.astype(jnp.bfloat16)
                return 0
            lax.fori_loop(0, bands, body, 0)

        @pl.when(is_in)
        def _():
            to_flat(24, 4)

        @pl.when(jnp.logical_not(is_in))
        def _():
            to_flat(6, 16)

        @pl.when(j == 0)
        def _():
            for load in loads:
                load.wait()

            @pl.when(me > 0)
            def _():
                for n, dst in enumerate((m_vm, v_vm, w_vm)):
                    frag_copy(n, dst).wait_recv()
                tail_copy().start()

        @pl.when(j == NCH - 1)
        def _():
            tail_sums()
        start = (base - shift) // 8 * 8

        def adam_body(i, _):
            adam_rows(start + i * 32, 32, True)
            return 0
        lax.fori_loop(0, CROWS // 32, adam_body, 0)
        adam_rows(start + CROWS, 8, False)

        @pl.when(is_in)
        def _():
            to_tiles(24, 4)

        @pl.when(jnp.logical_not(is_in))
        def _():
            to_tiles(6, 16)

        gather(j, me, wbuf.at[j], p_second, as_s.at[j], as_r.at[j]).start()
        gather(j, me, wbuf.at[j], p_first, af_s.at[j, 0], af_r.at[j, 0]).start()
        gather(j, me, wbuf.at[j], p_core, ac_s.at[j, 0], ac_r.at[j, 0]).start()
        pltpu.make_async_copy(wbuf.at[j], wb_all.at[me * NCH + j], wloc.at[j]).start()

        @pl.when(j >= 1)
        def _():
            for copy in out_copies(pl.multiple_of((j - 1) * CROWS, 8), CROWS, j - 1):
                copy.start()

    def stage_d(j):
        part = mine[1]
        gather(j, part, wbuf.at[j], p_second, as_s.at[j], as_r.at[j]).wait_recv()
        src = wb_all.at[part * NCH + j]
        gather(j, part, src, p_first, af_s.at[j, 1], af_r.at[j, 1]).start()
        gather(j, part, src, p_core, ac_s.at[j, 1], ac_r.at[j, 1]).start()

    def stage_e(j):
        for b in (0, 1):
            part = mine[2 + b]
            src = wb_all.at[part * NCH + j]
            gather(j, part, src, p_first, af_s.at[j, b], af_r.at[j, b]).wait_recv()
            gather(j, part, src, p_core, ac_s.at[j, 2 + b], ac_r.at[j, 2 + b]).start()

    def tail():
        start = (HEAD + PART - shift) // 8 * 8

        def body(i, _):
            adam_rows(start + i * 8, 8, True)
            return 0
        lax.fori_loop(0, (8544 - start) // 8, body, 0)

        @pl.when(me == 7)
        def _():
            wvec[...] = w_flat[pl.ds(HEAD + PART, 80), :].astype(jnp.bfloat16)
            for n in range(7):
                wvec_copy(n).start()
        for copy in out_copies((NCH - 1) * CROWS, OWN - (NCH - 1) * CROWS, NCH - 1):
            copy.start()

    offs = (0, 2, 4, 5, 6)

    def tick(t, _):
        for off, stage in zip(offs, (stage_a, stage_b, stage_c, stage_d, stage_e)):
            j = t - off

            @pl.when((j >= 0) & (j < NCH))
            def _():
                stage(j)
        @pl.when(t - offs[2] == NCH - 1)
        def _():
            tail()
        return 0
    lax.fori_loop(0, NCH + offs[-1], tick, 0)

    @pl.when(me < 7)
    def _():
        wvec_copy(0).wait_recv()
        for n, dst in enumerate((m_vm, v_vm, w_vm)):
            frag_copy(n, dst).wait_send()
        vec_copy(me).wait_send()

    @pl.when(me == 7)
    def _():
        for n in range(7):
            wvec_copy(n).wait_send()

    @pl.when(me > 0)
    def _():
        tail_copy().wait_send()
    wv_copy = pltpu.make_async_copy(wvec, wvec_out, wv_loc)
    wv_copy.start()

    def drain(j, _):
        for q in range(4):
            d2d(j, q, rc.at[j, q]).wait_send()
            gather(j, mine[q], wbuf.at[j], p_core, ac_s.at[j, q], ac_r.at[j, q]).wait()
        step_one(j).wait_send()
        step_two(j).wait_send()
        gather(j, me, wbuf.at[j], p_second, as_s.at[j], as_r.at[j]).wait_send()
        for b in (0, 1):
            gather(j, me, wbuf.at[j], p_first, af_s.at[j, b], af_r.at[j, b]).wait_send()
        pltpu.make_async_copy(wbuf.at[j], wb_all.at[me * NCH + j], wloc.at[j]).wait()
        return 0
    lax.fori_loop(0, NCH, drain, 0)

    def drain_out(j, _):
        for copy in out_copies(0, CROWS, j):
            copy.wait()
        return 0
    lax.fori_loop(0, NCH - 1, drain_out, 0)
    for copy in out_copies((NCH - 1) * CROWS, OWN - (NCH - 1) * CROWS, NCH - 1):
        copy.wait()
    wv_copy.wait()


def comm_call(grads, m_in, v_in, w_in, frag, vec):
    any_spec = pl.BlockSpec(memory_space=pl.ANY)
    f32, dma = jnp.float32, pltpu.SemaphoreType.DMA
    flat = jax.ShapeDtypeStruct((OWN, 128), f32)
    return pl.pallas_call(
        comm_kernel,
        out_shape=(flat, flat, flat,
                   jax.ShapeDtypeStruct((8 * NCH, TPC, 8, 128), jnp.bfloat16),
                   jax.ShapeDtypeStruct((80, 128), jnp.bfloat16)),
        in_specs=[any_spec] * 9,
        out_specs=[any_spec] * 5,
        scratch_shapes=[
            pltpu.VMEM((NCH, 4, TPC, 8, 128), f32),
            pltpu.VMEM((2, 4, TPC, 8, 128), f32),
            pltpu.VMEM((NCH, 2, TPC, 8, 128), f32),
            pltpu.VMEM((NCH, TPC, 8, 128), f32),
            pltpu.VMEM((8704, 128), f32),
            pltpu.VMEM((8704, 128), f32),
            pltpu.VMEM((8544, 128), f32),
            pltpu.VMEM((8544, 128), f32),
            pltpu.VMEM((8544, 128), f32),
            pltpu.VMEM((NCH, TPC, 8, 128), jnp.bfloat16),
            pltpu.VMEM((8, 80, 128), f32),
            pltpu.VMEM((80, 128), jnp.bfloat16),
            dma((NCH, 4)), dma((NCH, 4)), dma((2, 4)),
            dma((NCH,)), dma((NCH,)), dma((NCH,)), dma((NCH,)),
            dma((NCH,)), dma((NCH,)), dma((NCH, 2)), dma((NCH, 2)), dma((NCH, 4)), dma((NCH, 4)),
            dma((NCH,)), dma((3,)), dma((NCH, 3)),
            dma((3,)), dma((3,)), dma(()), dma(()), dma(()), dma((8,)), dma((7,)), dma(()), dma(()),
        ],
        compiler_params=pltpu.CompilerParams(collective_id=0, has_side_effects=True, vmem_limit_bytes=62 << 20),
        name="adam_exchange",
    )(*grads, m_in, v_in, w_in, frag, vec)


TM = 512
FCH = 512


def ffn_kernel(ids, act, emb_t, win, wout, b_in, b_out, y_ref, table, rows):
    @pl.when(pl.program_id(0) == 0)
    def _():
        def fill(b, _):
            for c in range(6):
                tile = emb_t[b * 6 + c].astype(jnp.float32) * math.sqrt(D)
                table[pl.ds(b * 64 + c, 8, stride=8), :] = tile
            return 0
        lax.fori_loop(0, VOCAB // 8, fill, 0)

    def pick(i, _):
        for k in range(16):
            r = i * 16 + k
            tok = ids[0, 0, r]
            rows[pl.ds(pl.multiple_of(r * 8, 8), 8), :] = table[pl.ds(pl.multiple_of(tok * 8, 8), 8), :]
        return 0
    lax.fori_loop(0, TM // 16, pick, 0)
    h = jnp.concatenate(
        [(rows[pl.ds(c, TM, stride=8), :] + act[:, c * 128:(c + 1) * 128].astype(jnp.float32)).astype(jnp.bfloat16)
         for c in range(6)], axis=1)
    inner = []
    for f in range(FF // FCH):
        at = slice(f * FCH, (f + 1) * FCH)
        pre = jnp.dot(h, win[:, at], preferred_element_type=jnp.float32) + b_in[:, at].astype(jnp.float32)
        inner.append(jax.nn.gelu(pre, approximate=True).astype(jnp.bfloat16))
    u = jnp.concatenate(inner, axis=1)
    out = jnp.dot(u, wout[...], preferred_element_type=jnp.float32) + b_out[...].astype(jnp.float32)
    y_ref[...] = out.astype(jnp.bfloat16)


def ffn_call(tok_ids, act_in, emb_t, win, wout, b_in, b_out):
    steps = act_in.shape[0] // TM
    const = lambda shape: pl.BlockSpec(shape, lambda i: (0,) * len(shape), pipeline_mode=pl.Buffered(1))
    return pl.pallas_call(
        ffn_kernel,
        grid=(steps,),
        out_shape=jax.ShapeDtypeStruct(act_in.shape, jnp.bfloat16),
        in_specs=[
            pl.BlockSpec((1, 1, TM), lambda i: (i, 0, 0), memory_space=pltpu.SMEM),
            pl.BlockSpec((TM, D), lambda i: (i, 0)),
            const((VOCAB * D // 1024, 8, 128)), const((D, FF)), const((FF, D)), const((1, FF)), const((1, D)),
        ],
        out_specs=pl.BlockSpec((TM, D), lambda i: (i, 0)),
        scratch_shapes=[pltpu.VMEM((VOCAB * 8, 128), jnp.float32), pltpu.VMEM((TM * 8, 128), jnp.float32)],
        compiler_params=pltpu.CompilerParams(dimension_semantics=("arbitrary",), vmem_limit_bytes=62 << 20),
        name="gather_ffn",
    )(tok_ids.reshape(steps, 1, TM), act_in, emb_t, win, wout, b_in, b_out)


def to_tiles(arr):
    rows, cols = arr.shape
    return arr.reshape(rows // 8, 8, cols // 128, 128).transpose(0, 2, 1, 3).reshape(rows * cols // 1024, 8, 128)


def from_tiles(tiles, rows, cols):
    return tiles.reshape(rows // 8, cols // 128, 8, 128).transpose(0, 2, 1, 3).reshape(rows, cols)


def solution(mesh):
    def device_step(g_emb, g_attn, g_in, g_out, g_vecd, g_vecf, opt_m, opt_v, master, tok_ids, act_in):
        grads = [to_tiles(g_emb[0]), to_tiles(g_attn.reshape(4 * D, D)), to_tiles(g_in[0, 0]), to_tiles(g_out[0, 0])]
        vec = jnp.concatenate([g_vecd.reshape(-1), g_vecf.reshape(-1), jnp.zeros((256,), jnp.float32)]).reshape(80, 128)
        state = [opt_m, opt_v, master]
        frag = jnp.concatenate([arr[-HEAD * 128:] for arr in state]).reshape(3 * HEAD, 128)
        m_new, v_new, w_new, wb_all, wvec = comm_call(grads, *[arr.reshape(OWN, 128) for arr in state], frag, vec)
        tiles = [wb_all[BOUNDS[n]:BOUNDS[n + 1]].reshape(-1, 8, 128) for n in range(4)]
        wb_emb = from_tiles(tiles[0], VOCAB, D)
        wb_attn = from_tiles(tiles[1], 4 * D, D).reshape(1, 4, D, D)
        wb_in = from_tiles(tiles[2], D, FF)
        wb_out = from_tiles(tiles[3], FF, D)
        vec_flat = wvec.reshape(-1)
        wb_vecd = vec_flat[:9 * D].reshape(1, 9, D)
        wb_vecf = vec_flat[9 * D:9 * D + FF].reshape(1, FF)
        y_out = ffn_call(tok_ids, act_in, tiles[0], wb_in, wb_out, wb_vecf, wb_vecd[0, 8:9])
        return (m_new.reshape(-1), v_new.reshape(-1), w_new.reshape(-1), wb_emb, wb_attn, wb_in[None], wb_out[None],
                wb_vecd, wb_vecf, y_out)

    grad_specs = tuple(P(AXES, *([None] * (grad_rank - 1))) for grad_rank in GRAD_RANKS)
    in_specs = grad_specs + (P(AXES), P(AXES), P(AXES), P(AXES), P(AXES, None))
    out_specs = (P(AXES), P(AXES), P(AXES), P(), P(), P(), P(), P(), P(), P(AXES, None))
    return jax.shard_map(device_step, mesh=mesh, in_specs=in_specs, out_specs=out_specs, check_vma=False)
```

time: 1420 us -> 462 us (0.33)
  waiting for transfers between devices: 562 us -> 0 us
  Pallas kernels: 0 us -> 429 us
  other arithmetic: 346 us -> 2.8 us
  local copies, waits for them, and re-layouts: 263 us -> 29.1 us
  matrix products: 224 us -> 0 us
    pallas_call x0 -> x2, Pallas kernels: none -> 429 us  [the longest x1 223 us: comm_call(): pl.pallas_call(comm_kernel, out_shape=(flat, flat, flat, jax.ShapeDtypeSt...]
    unnamed x3 -> x0, waiting for transfers between devices: 401 us -> none
    all_gather x1 -> x0, other arithmetic: 334 us -> none  [device_step(): lax.all_gather(w_new.astype(jnp.bfloat16), AXES, axis=0, tiled=True)]
    dot_general x2 -> x0, matrix products: 224 us -> none  [the longest x1 136 us: ffn_block(): jnp.dot(hidden, w_in, preferred_element_type=jnp.float32)]
    all_gather x1 -> x0, waiting for transfers between devices: 161 us -> none  [device_step(): lax.all_gather(w_new.astype(jnp.bfloat16), AXES, axis=0, tiled=True)]
    unnamed x18 -> x11, local copies, waits for them, and re-layouts: 90.3 us -> 11.5 us
    gather x1 -> x0, local copies, waits for them, and re-layouts: 67.8 us -> none  [ffn_block(): emb_rows = jnp.take(wb_emb, tok_ids, axis=0).astype(jnp.float32)]
    reshape x10 -> x2, local copies, waits for them, and re-layouts: 61.2 us -> 0.04 us  [the longest x1 0.04 us: device_step(): wb_vecd = vec_flat[:9 * D].reshape(1, 9, D)]
  transfers between devices with their start and end apart: 2 -> 0, of which waited for: 2 -> 0; matrix products, arithmetic and copies ran while one was open for 0% -> 0% of each run, Pallas kernels for 0% -> 0%
where the time goes in v1:
time: 462 us; the launch traced here: 461 us
  Pallas kernels  429 us (93%)
  local copies, waits for them, and re-layouts  29.1 us (6%)
    pallas_call x1, Pallas kernels, comm_call(): pl.pallas_call(comm_kernel, out_shape=(flat, flat, flat, jax.ShapeDtypeSt...  223 us
    pallas_call x1, Pallas kernels, ffn_call(): pl.pallas_call(ffn_kernel, grid=(steps,), out_shape=jax.ShapeDtypeStruct(...  206 us
    slice x2, local copies, waits for them, and re-layouts, device_step(): wb_all[BOUNDS[n]:BOUNDS[n + 1]].reshape(-1, 8, 128)  14.6 us
    unnamed x11, local copies, waits for them, and re-layouts  11.5 us

profile of v1, /device:TPU:0, one launch (start us, length us, event | category | flops | bytes accessed | tf_op | source)
XLA Modules:
  0.0 461.5 jit_solution(17084067643503105386)
XLA Ops:
  0.6 0.8 slice_bitcast_fusion.2
  1.4 0.8 reduce
  2.3 1.3 maximum_bitcast_fusion.vec
  3.6 0.8 slice_bitcast_fusion
  4.4 0.7 pad_maximum_fusion.frag
  5.1 222.9 %adam_exchange.1 = (f32[8458,128]{1,0:T(8,128)}, f32[8458,128]{1,0:T(8,128)}, f32[8458,128]{1,0:T(8,128)}, bf16[88,96,8,128]{3,2,1,0:T(8,128)(2,1)}, bf16[80,128]{1,0:T(8,128)(2,1)}) custom-call(f32[1536,8,128]{2,1,0:T(8,128)} %bitcast.78, f32[2304,8,128]{2,1,0:T(8,128)} %bitcast.75, f32[2304,8,128]{2,1,0:T(8,128)} %bitcast.76, f32[2304,8,128]{2,1,0:T(8,128)} %bitcast.77, ...), custom_call_target="tpu_custom_call" | custom-call | tf_op jit(solution)/shard_map/adam_exchange/pallas_call | solution.py:367
  228.0 0.7 slice_bitcast_fusion.3
  228.7 0.7 slice.72
  229.5 0.6 copy.23
  230.1 0.0 copy-start
  230.1 0.6 slice_bitcast_fusion.4.b_out
  230.7 3.9 slice.68
  234.6 10.8 %fusion = (bf16[24,96,8,128]{3,2,1,0:T(8,128)(2,1)}, bf16[24,96,8,128]{3,2,1,0:T(8,128)(2,1)}, bf16[24,96,8,128]{3,2,1,0:T(8,128)(2,1)}) fusion(bf16[88,96,8,128]{3,2,1,0:T(8,128)(2,1)} %get-tuple-element.18), kind=kLoop, calls=%fused_computation.8 | loop fusion | bytes 28311552 | tf_op jit(solution)/shard_map/slice | solution.py:467
  245.3 0.0 copy-done
  245.3 206.0 %gather_ffn.1 = bf16[16384,768]{1,0:T(8,128)(2,1)} custom-call(s32[32,1,512]{2,1,0:T(1,128)} %bitcast.88, bf16[16384,768]{1,0:T(8,128)(2,1)} %act.1, bf16[1536,8,128]{2,1,0:T(8,128)(2,1)} %bitcast.73, bf16[768,3072]{1,0:T(8,128)(2,1)} %bitcast.71, bf16[3072,768]{1,0:T(8,128)(2,1)} %bitcast.69, bf16[1,3072]{1,0:T(2,128)(2,1)} %bitcast.89, ...), custom_call_target="tpu_custom_call" | custom-call | tf_op jit(solution)/shard_map/gather_ffn/pallas_call | solution.py:435
  451.3 0.0 slice-start
  451.3 4.1 copy.27
  455.4 0.0 slice-start.1
  455.4 3.8 copy.28
  459.3 0.0 slice-done
  459.3 0.0 slice-done.1
  459.3 2.2 copy.29
  (4 shorter events, 0.0 us)
Async XLA Ops:
  230.1 15.2 %copy-start = (bf16[1,9,768]{2,1,0:T(8,128)(2,1)}, bf16[1,9,768]{2,1,0:T(8,128)(2,1)S(1)}, u32[]{:S(2)}) copy-start(bf16[1,9,768]{2,1,0:T(8,128)(2,1)S(1)} %reshape.127) | copy-start | bytes 41476
  451.3 8.0 %slice-start = ((s8[4333568]{0:T(1024)(128)(4,1)}), s8[4194304]{0:T(1024)(128)(4,1)S(1)}, s32[]{:S(2)}) async-start(s8[4333568]{0:T(1024)(128)(4,1)} %bitcast.83), calls=%async_computation | async-start | bytes 8388608
  455.4 3.9 slice-start.1
